TPU v7x, 32 devices: a whole 2x2x4 slice. The times are simulated.
32 devices in a mesh: aper: 4 (over y, x), rng: 4 (over z), beam: 2 (over core).
Axes of the slice: x: 2, y: 2, z: 4, core: 2. Of those that a mesh axis runs over, the one named last changes fastest.
Arguments:
- children: float32 [4, 2, 8192, 256], P('aper', None, 'rng', 'beam'), may hold values from -6 to 6
- shift_one: int32 [2, 256], replicated, may hold values from -8 to 8
- rtaps_one: float32 [2, 8, 256], replicated, may hold values from -2 to 2
- bstart_one: int32 [2, 512], replicated, may hold values from -5 to 252, as said below
- btaps_one: float32 [2, 8, 512], replicated, may hold values from -2 to 2
- prate_one: float32 [2, 512], replicated, may hold values from -64 to 64
- poff_one: float32 [2, 512], replicated, may hold values from -3.140625 to 3.140625
- shift_two: int32 [2, 512], replicated, may hold values from -8 to 8
- rtaps_two: float32 [2, 8, 512], replicated, may hold values from -2 to 2
- bstart_two: int32 [2, 1024], replicated, may hold values from -5 to 508, as said below
- btaps_two: float32 [2, 8, 1024], replicated, may hold values from -2 to 2
- prate_two: float32 [2, 1024], replicated, may hold values from -64 to 64
- poff_two: float32 [2, 1024], replicated, may hold values from -3.140625 to 3.140625
Outputs:
- merged: float32 [4, 2, 8192, 256], P('aper', None, 'rng', 'beam')
Inputs may be any that keep to these rules, and one draw needn't show every extreme that they name: bstart_one[c, b] is b // 2 - 8 // 2 plus -1, 0 or 1. bstart_two[c, b] is b // 2 - 8 // 2 plus -1, 0 or 1.
All inputs are finite; a program needn't handle non-finite values.
Results may differ from a plain program's by a relative error of at most 0.0003.
Values sent between devices are 32-bit elements; how exact they have to be, the bound alone decides.
No kernel may reach another device: no remote copies, remote signals or barrier semaphores. Data moves between devices by JAX's collectives and lax.ppermute only.
A program may use at most 64 MiB of HBM per device.

v0:
```python
import functools

import jax
import jax.numpy as jnp
from jax import lax
from jax.experimental import pallas as pl
from jax.experimental.pallas import tpu as pltpu
from jax.sharding import PartitionSpec as P


TAPS = 8
SPAN = 8
GROUP = 4
TILE = 128
RIM = 8
PRIM = 5
HALO = 16
FINE = 2 * TAPS - 1
ANY = pl.BlockSpec(memory_space=pl.ANY)
HBM = pl.BlockSpec(memory_space=pltpu.HBM)
SMEM = pl.BlockSpec(memory_space=pltpu.SMEM)
VMEM = pl.BlockSpec(memory_space=pltpu.VMEM)
F32 = jnp.float32
BF16 = jnp.bfloat16
PARAMS = pltpu.CompilerParams(vmem_limit_bytes=24 << 20)


def plan_of(tiles):
    quarter = tiles // 4
    half = quarter // 2
    ring = list(range(tiles - half, tiles)) + list(range(tiles - half))
    return [ring[i * quarter : (i + 1) * quarter] for i in range(4)]


def spans(tiles):
    runs = []
    for position, tile in enumerate(tiles):
        if runs and tile == runs[-1][1] + runs[-1][2]:
            runs[-1][2] += 1
        else:
            runs.append([position, tile, 1])
    return runs


def lanes(tile, count=1):
    return pl.ds(tile * TILE, count * TILE)


def fetch(child, rows_in, first, count, sem):
    rows = pl.ds(first * TILE, count * TILE)
    return pltpu.make_async_copy(child.at[0, :, rows, :], rows_in.at[:, rows, :], sem)


def first_pack(plan, sc, child, *refs):
    outs, (rows_in, turned, sem) = refs[:3], refs[3:]
    sub = child.shape[3] // GROUP
    runs = spans(plan[0])
    copies = [fetch(child, rows_in, first, count, sem) for _, first, count in runs]
    for copy in copies:
        copy.start()
    for copy in copies:
        copy.wait()
    for position, tile in enumerate(plan[0]):
        for part in range(2):
            turned[part, :, lanes(position)] = rows_in[part, lanes(tile), :].T
    for k in range(1, GROUP):
        start = pl.multiple_of(jnp.bitwise_xor(sc[0], k) * sub, 8)
        for part in range(2):
            outs[k - 1][part] = turned[part, pl.ds(start, sub), :]


def turn_all(sc, child, after, rim, turned, rows_in, sems):
    del after
    blk = child.shape[3]
    tiles = child.shape[2] // TILE
    step = tiles // 4
    copies = [fetch(child, rows_in, i * step, step, sems.at[i]) for i in range(4)]
    for copy in copies:
        copy.start()
    for i, copy in enumerate(copies):
        copy.wait()

        def turn(j, carry):
            tile = i * step + j
            for part in range(2):
                turned[part, :, lanes(tile)] = rows_in[part, lanes(tile), :].T
            return carry

        lax.fori_loop(0, step, turn, 0, unroll=2)
    side = pl.multiple_of((1 - sc[1]) * (blk - RIM), 8)
    for part in range(2):
        rim[part] = turned[part, pl.ds(side, RIM), :]


def second_pack(plan, sc, turned, rim, *refs):
    outs, (own, full) = refs[:9], refs[9:]
    blk = turned.shape[1]
    sub = blk // GROUP
    wide = sub + 2 * RIM
    upper = sc[1] != 0
    for part in range(2):
        full[part, pl.ds(0, RIM), :] = jnp.where(upper, rim[part], 0.0)
        full[part, pl.ds(RIM, blk), :] = turned[part]
        full[part, pl.ds(RIM + blk, RIM), :] = jnp.where(upper, 0.0, rim[part])
    for part in range(2):
        own[part] = full[part, pl.ds(pl.multiple_of(sc[0] * sub, 8), wide), :]
        for k in range(1, GROUP):
            start = pl.multiple_of(jnp.bitwise_xor(sc[0], k) * sub, 8)
            for step in range(1, 4):
                target = outs[3 * (step - 1) + k - 1]
                for position, first, count in spans(plan[step]):
                    target[part, pl.ds(0, wide), lanes(position, count)] = full[
                        part, pl.ds(start, wide), lanes(first, count)
                    ]
                if step == 1:
                    for position, first, count in spans(plan[0]):
                        for at, row in ((wide, start), (wide + RIM, start + RIM + sub)):
                            target[part, pl.ds(at, RIM), lanes(position, count)] = full[
                                part, pl.ds(pl.multiple_of(row, 8), RIM), lanes(first, count)
                            ]


def raw_beams(plan, sub, own, low, high, remote, k, part, tile):
    wide = sub + 2 * RIM
    tiles = own.shape[2] // TILE
    if tile < 0:
        return low[k, part]
    if tile >= tiles:
        return high[k, part]
    if k == 0:
        return own[part, :, lanes(tile)]
    step = next(i for i in range(4) if tile in plan[i])
    at = plan[step].index(tile)
    if step > 0:
        return remote[step][k - 1][part, pl.ds(0, wide), lanes(at)]
    rims = remote[1][k - 1]
    return jnp.concatenate(
        [
            rims[part, pl.ds(wide, RIM), lanes(at)],
            remote[0][k - 1][part, :, lanes(at)],
            rims[part, pl.ds(wide + RIM, RIM), lanes(at)],
        ],
        axis=0,
    )


def edge_pack(plan, sub, own, *refs):
    remote = {0: refs[:3], 1: refs[3:6]}
    to_high, to_low = refs[6:]
    tiles = own.shape[2] // TILE
    for target, tile in ((to_high, tiles - 1), (to_low, 0)):
        for k in range(GROUP):
            for part in range(2):
                target[k, part] = raw_beams(plan, sub, own, None, None, remote, k, part, tile)


def spread(load, store_to, rows, table):
    coarse = table[FINE : FINE + 1, :]
    near, far = coarse == 1.0, coarse == 2.0
    step = 64
    for start in range(0, rows, step):
        size = min(step, rows - start)
        store_to[pl.ds(start, size), :] = jnp.where(
            far, load(start + 16, size), jnp.where(near, load(start + 8, size), load(start, size))
        )


def fine_taps(shifted, start, size, table):
    total = None
    for tap in range(FINE):
        term = table[tap : tap + 1, :] * shifted[pl.ds(start + tap + 4, size), :]
        total = term if total is None else total + term
    return total


def split_into(lhs, at, size, value):
    high = value.astype(BF16)
    low = (value - high.astype(F32)).astype(BF16)
    lhs[pl.ds(at, size), pl.ds(0, TILE)] = high
    lhs[pl.ds(at, size), pl.ds(TILE, TILE)] = low


def turn_factor(base, fine, side, block, start, size):
    base_cos = base[side, 0, pl.ds(block, 1), :]
    base_sin = base[side, 1, pl.ds(block, 1), :]
    fine_cos = fine[side, 0, pl.ds(start, size), :]
    fine_sin = fine[side, 1, pl.ds(start, size), :]
    return base_cos * fine_cos - base_sin * fine_sin, base_sin * fine_cos + base_cos * fine_sin


def merge(plan, steps, runs, sub, has_edges, keep, sc, *refs):
    refs = list(refs)
    own = refs.pop(0)
    low = refs.pop(0) if has_edges else None
    high = refs.pop(0) if has_edges else None
    remote = {}
    for step in steps:
        remote[step] = refs[:3]
        del refs[:3]
    (taps_one, mats_one, lows_one, base_one, fine_one, taps_two, mats_two, base_two, fine_two) = refs[:9]
    del refs[:9]
    if keep:
        refs.pop(0)
    out, flat, shifted, lhs, mixed, parent, done, out_sem = refs
    tiles = own.shape[2] // TILE
    row_base, rows_total = sc[2], sc[3]
    wide = sub + 2 * RIM
    half = TILE // 2
    blank = jnp.zeros((half - wide, TILE), F32)
    results = []
    done_at = 0
    for first, count in runs:
        for i in range(count + 2):
            for side in range(2):
                for part in range(2):
                    pair = [
                        raw_beams(plan, sub, own, low, high, remote, 2 * side + j, part, first - 1 + i)
                        for j in range(2)
                    ]
                    flat[side, part, lanes(i), :] = jnp.concatenate(
                        [pair[0], blank, pair[1], blank], axis=0
                    ).T
        edges = first == 0 or first + count == tiles

        def parent_block(i, rows):
            for side in range(2):
                for part in range(2):

                    def load(start, size):
                        return flat[
                            side, part, pl.ds(pl.multiple_of(i * TILE + TILE - 2 * HALO + start, 8), size), :
                        ]

                    spread(load, shifted.at[side, part], rows + 24, taps_one[side])
                    for start in range(0, rows, min(rows, half)):
                        size = min(rows, half)
                        split_into(
                            lhs.at[side],
                            part * rows + start,
                            size,
                            fine_taps(shifted.at[side, part], start, size, taps_one[side]),
                        )
                both = pl.ds(0, 2 * rows)
                mixed[side, both, :] = jnp.dot(
                    lhs[side, both, :], mats_one[side], preferred_element_type=F32
                ) + jnp.dot(lhs[side, both, pl.ds(0, TILE)], lows_one[side], preferred_element_type=F32)
            size = min(rows, 32)
            for start in range(0, rows, size):
                sums = [[None, None], [None, None]]
                for side in range(2):
                    cosine, sine = turn_factor(base_one, fine_one, side, first + i, start, size)
                    if edges:
                        row = (
                            lax.broadcasted_iota(jnp.int32, (size, TILE), 0)
                            + row_base
                            + (first + i) * TILE
                            - HALO
                            + start
                        )
                        valid = jnp.logical_and(row >= 0, row < rows_total)
                        cosine = jnp.where(valid, cosine, 0.0)
                        sine = jnp.where(valid, sine, 0.0)
                    for image in range(2):
                        beams = pl.ds(image * TILE, TILE)
                        real = mixed[side, pl.ds(start, size), beams]
                        imag = mixed[side, pl.ds(rows + start, size), beams]
                        terms = (cosine * real - sine * imag, sine * real + cosine * imag)
                        for part in range(2):
                            have = sums[image][part]
                            sums[image][part] = terms[part] if have is None else have + terms[part]
                for image in range(2):
                    for part in range(2):
                        parent[image, part, pl.ds(pl.multiple_of(i * TILE + start, 8), size), :] = sums[
                            image
                        ][part]

        def full_block(i, carry):
            parent_block(i, TILE)
            return carry

        lax.fori_loop(0, count, full_block, 0)
        parent_block(count, 2 * HALO)
        parent[:, :, pl.ds(count * TILE + 2 * HALO, 16), :] = jnp.zeros((2, 2, 16, TILE), F32)

        def final_block(i, carry):
            for image in range(2):
                for part in range(2):

                    def load(start, size):
                        return parent[image, part, pl.ds(pl.multiple_of(i * TILE + start, 8), size), :]

                    spread(load, shifted.at[image, part], TILE + 24, taps_two[image])
                    for start in range(0, TILE, half):
                        split_into(
                            lhs.at[image],
                            part * TILE + start,
                            half,
                            fine_taps(shifted.at[image, part], start, half, taps_two[image]),
                        )
                mixed[image] = jnp.dot(lhs[image], mats_two[image], preferred_element_type=F32)
            size = 32
            for start in range(0, TILE, size):
                sums = [None, None]
                for image in range(2):
                    cosine, sine = turn_factor(base_two, fine_two, image, first + i, start, size)
                    real, imag = (
                        mixed[image, pl.ds(part * TILE + start, size), pl.ds(0, TILE)]
                        + mixed[image, pl.ds(part * TILE + start, size), pl.ds(TILE, TILE)]
                        for part in range(2)
                    )
                    terms = (cosine * real - sine * imag, sine * real + cosine * imag)
                    for part in range(2):
                        sums[part] = terms[part] if sums[part] is None else sums[part] + terms[part]
                for part in range(2):
                    done[part, pl.ds(pl.multiple_of((done_at + i) * TILE + start, 8), size), :] = sums[part]
            return carry

        lax.fori_loop(0, count, final_block, 0)
        result = pltpu.make_async_copy(
            done.at[:, lanes(done_at, count), :], out.at[0, :, lanes(first, count), :], out_sem
        )
        result.start()
        results.append(result)
        done_at += count
    for result in results:
        result.wait()


def make_tables(
    sub,
    sc,
    shift_one,
    rtaps_one,
    bstart_one,
    btaps_one,
    prate_one,
    poff_one,
    shift_two,
    rtaps_two,
    bstart_two,
    btaps_two,
    prate_two,
    poff_two,
    taps_one,
    mats_one,
    lows_one,
    base_one,
    fine_one,
    taps_two,
    mats_two,
    base_two,
    fine_two,
):
    mine, beam, row_base = sc[0], sc[1], sc[2]
    total = sc[3].astype(F32)
    block = GROUP * beam + mine
    half = TILE // 2
    child_first = sub * block - RIM
    parent_first = 2 * sub * block - PRIM
    final_first = 4 * sub * block
    lane = lax.broadcasted_iota(jnp.int32, (TAPS, TILE), 1)

    def windowed(rows, first):
        count = rows.shape[1]
        moved = pltpu.roll(rows, lax.rem(2 * count - first, count), 1)[:, :TILE]
        spot = lane + first
        return jnp.where(jnp.logical_and(spot >= 0, spot < count), moved, jnp.zeros_like(moved))

    def line(table, side, first):
        return windowed(jnp.broadcast_to(table[pl.ds(side, 1), :], (TAPS, table.shape[1])), first)

    def twice(rows):
        return jnp.where(lane < half, rows, pltpu.roll(rows, half, 1))

    def range_table(target, shifts, taps):
        moved = shifts[0:1, :] + SPAN
        spot = lax.broadcasted_iota(jnp.int32, (2 * TAPS, TILE), 0)
        apart = spot - lax.rem(moved, jnp.int32(TAPS))
        total_rows = jnp.zeros((2 * TAPS, TILE), F32)
        for k in range(TAPS):
            total_rows = total_rows + jnp.where(apart == k, taps[k : k + 1, :], 0.0)
        target[...] = jnp.where(spot == FINE, (moved // TAPS).astype(F32), total_rows)

    def beam_matrix(starts, taps, first, height):
        apart = lax.broadcasted_iota(jnp.int32, (height, TILE), 0) - (starts[0:1, :] - first)
        matrix = jnp.zeros((height, TILE), F32)
        for k in range(TAPS):
            matrix = matrix + jnp.where(apart == k, taps[k : k + 1, :], 0.0)
        high = matrix.astype(BF16)
        return high, (matrix - high.astype(F32)).astype(BF16)

    def turn_tables(base, fine, rates, offsets, row_first):
        rate, offset = rates[0:1, :], offsets[0:1, :]
        blocks = base.shape[1]
        start = lax.broadcasted_iota(jnp.int32, (blocks, TILE), 0) * TILE + row_first
        angle = rate * (start.astype(F32) / total) + offset
        base[0] = jnp.cos(angle)
        base[1] = jnp.sin(angle)
        groups = TILE // 8
        coarse = rate * ((lax.broadcasted_iota(jnp.int32, (groups, TILE), 0) * 8).astype(F32) / total)
        small = rate * (lax.broadcasted_iota(jnp.int32, (8, TILE), 0).astype(F32) / total)
        coarse_cos, coarse_sin = jnp.cos(coarse), jnp.sin(coarse)
        small_cos, small_sin = jnp.cos(small), jnp.sin(small)
        for j in range(groups):
            cosine, sine = coarse_cos[j : j + 1, :], coarse_sin[j : j + 1, :]
            fine[0, pl.ds(8 * j, 8), :] = cosine * small_cos - sine * small_sin
            fine[1, pl.ds(8 * j, 8), :] = sine * small_cos + cosine * small_sin

    for slot in range(2):
        side = jnp.bitwise_xor(mine // 2, slot)
        range_table(
            taps_one.at[slot],
            twice(line(shift_one, side, child_first)),
            twice(windowed(rtaps_one[side], child_first)),
        )
        high, low = beam_matrix(
            line(bstart_one, side, parent_first),
            windowed(btaps_one[side], parent_first),
            child_first,
            half,
        )
        for target, value, copies in ((mats_one, high, 2), (lows_one, low, 1)):
            none = jnp.zeros_like(value)
            for i in range(copies):
                target[slot, pl.ds(i * TILE, half), pl.ds(0, TILE)] = value
                target[slot, pl.ds(i * TILE, half), pl.ds(TILE, TILE)] = none
                target[slot, pl.ds(i * TILE + half, half), pl.ds(0, TILE)] = none
                target[slot, pl.ds(i * TILE + half, half), pl.ds(TILE, TILE)] = value
        turn_tables(
            base_one.at[slot],
            fine_one.at[slot],
            line(prate_one, side, parent_first),
            line(poff_one, side, parent_first),
            row_base - HALO,
        )
        side = jnp.bitwise_xor(mine % 2, slot)
        range_table(
            taps_two.at[slot],
            line(shift_two, side, parent_first),
            windowed(rtaps_two[side], parent_first),
        )
        high, low = beam_matrix(
            line(bstart_two, side, final_first),
            windowed(btaps_two[side], final_first),
            parent_first,
            TILE,
        )
        mats_two[slot, pl.ds(0, TILE), pl.ds(0, TILE)] = high
        mats_two[slot, pl.ds(0, TILE), pl.ds(TILE, TILE)] = low
        mats_two[slot, pl.ds(TILE, TILE), pl.ds(0, TILE)] = high
        mats_two[slot, pl.ds(TILE, TILE), pl.ds(TILE, TILE)] = jnp.zeros_like(high)
        turn_tables(
            base_two.at[slot],
            fine_two.at[slot],
            line(prate_two, side, final_first),
            line(poff_two, side, final_first),
            row_base,
        )


def body(
    children,
    shift_one,
    rtaps_one,
    bstart_one,
    btaps_one,
    prate_one,
    poff_one,
    shift_two,
    rtaps_two,
    bstart_two,
    btaps_two,
    prate_two,
    poff_two,
):
    rows, blk = children.shape[2], children.shape[3]
    sub = blk // GROUP
    wide = sub + 2 * RIM
    tiles = rows // TILE
    apers, beams = lax.axis_size("aper"), lax.axis_size("beam")
    total = rows * lax.axis_size("rng")
    assert children.shape[0] == 1 and beams == 2 and apers % GROUP == 0
    assert blk == TILE and rows % (8 * TILE) == 0
    plan = plan_of(tiles)
    mine = lax.axis_index("aper") % GROUP
    beam = lax.axis_index("beam")
    row_base = lax.axis_index("rng") * rows
    sc = jnp.stack([mine, beam, row_base, jnp.int32(total)]).astype(jnp.int32)

    def out(*shape):
        return pltpu.VMEM(shape, F32)

    def near(arrays):
        return [pltpu.with_memory_space_constraint(array, pltpu.VMEM) for array in arrays]

    def call(kernel, *operands, **settings):
        return pl.pallas_call(kernel, compiler_params=PARAMS, **settings)(*operands)

    def swap(block, k):
        return lax.ppermute(block, "aper", [(i, i ^ k) for i in range(apers)])

    children = pltpu.with_memory_space_constraint(children, pltpu.HBM)
    widths = [len(part) * TILE for part in plan]
    edge = call(
        functools.partial(first_pack, plan),
        sc, children,
        out_shape=[out(2, sub, widths[0])] * 3,
        in_specs=[SMEM, HBM],
        out_specs=[VMEM] * 3,
        scratch_shapes=[
            pltpu.VMEM((2, rows, blk), F32),
            pltpu.VMEM((2, blk, widths[0]), F32),
            pltpu.SemaphoreType.DMA,
        ],
    )
    remote = {0: [swap(edge[k - 1], k) for k in range(1, GROUP)]}
    rim, turned = call(
        turn_all,
        sc, children, edge[0],
        out_shape=[out(2, RIM, rows), out(2, blk, rows)],
        in_specs=[SMEM, HBM, ANY],
        out_specs=[VMEM] * 2,
        scratch_shapes=[pltpu.VMEM((2, rows, blk), F32), pltpu.SemaphoreType.DMA((4,))],
    )
    rim = lax.ppermute(rim, "beam", [(0, 1), (1, 0)])
    *packed, own = call(
        functools.partial(second_pack, plan),
        sc, *near([turned, rim]),
        out_shape=[out(2, wide + 2 * RIM, widths[1])] * 3
        + [out(2, wide, widths[2])] * 3
        + [out(2, wide, widths[3])] * 3
        + [out(2, wide, rows)],
        in_specs=[SMEM, VMEM, VMEM],
        out_specs=[VMEM] * 10,
        scratch_shapes=[pltpu.VMEM((2, blk + 2 * RIM, rows), F32)],
    )
    for step in range(1, 4):
        remote[step] = [swap(packed[3 * (step - 1) + k - 1], k) for k in range(1, GROUP)]

    to_high, to_low = call(
        functools.partial(edge_pack, plan, sub),
        *near([own, *remote[0], *remote[1]]),
        out_shape=[out(GROUP, 2, wide, TILE)] * 2,
        in_specs=[VMEM] * 7,
        out_specs=[VMEM] * 2,
    )
    ranks = lax.axis_size("rng")
    low = lax.ppermute(to_high, "rng", [(i, i + 1) for i in range(ranks - 1)])
    high = lax.ppermute(to_low, "rng", [(i + 1, i) for i in range(ranks - 1)])

    def brief(*shape):
        return pltpu.VMEM(shape, BF16)

    blocks = tiles + 8
    given = (
        shift_one,
        rtaps_one,
        bstart_one,
        btaps_one,
        prate_one,
        poff_one,
        shift_two,
        rtaps_two,
        bstart_two,
        btaps_two,
        prate_two,
        poff_two,
    )
    tables = call(
        functools.partial(make_tables, sub),
        sc, *given,
        out_shape=[
            out(2, 2 * TAPS, TILE),
            brief(2, 2 * TILE, 2 * TILE),
            brief(2, TILE, 2 * TILE),
            out(2, 2, blocks, TILE),
            out(2, 2, TILE, TILE),
            out(2, 2 * TAPS, TILE),
            brief(2, 2 * TILE, 2 * TILE),
            out(2, 2, blocks, TILE),
            out(2, 2, TILE, TILE),
        ],
        in_specs=[SMEM] + [VMEM] * len(given),
        out_specs=[VMEM] * 9,
    )

    def merged(steps, runs, use_edges, before):
        arrays = [own] + ([low, high] if use_edges else [])
        for step in steps:
            arrays += remote[step]
        longest = max(count for _, count in runs)
        keep = before is not None
        operands = [sc, *near([*arrays, *tables])] + ([before] if keep else [])
        return call(
            functools.partial(merge, plan, steps, runs, sub, use_edges, keep),
            *operands,
            out_shape=jax.ShapeDtypeStruct((1, 2, rows, blk), F32),
            in_specs=[SMEM] + [VMEM] * (len(arrays) + len(tables)) + ([ANY] if keep else []),
            out_specs=ANY,
            input_output_aliases={len(operands) - 1: 0} if keep else {},
            scratch_shapes=[
                pltpu.VMEM((2, 2, (longest + 2) * TILE, TILE), F32),
                pltpu.VMEM((2, 2, TILE + 24, TILE), F32),
                pltpu.VMEM((2, 2 * TILE, 2 * TILE), BF16),
                pltpu.VMEM((2, 2 * TILE, 2 * TILE), F32),
                pltpu.VMEM((2, 2, longest * TILE + 2 * HALO + 16, TILE), F32),
                pltpu.VMEM((2, sum(count for _, count in runs) * TILE, TILE), F32),
                pltpu.SemaphoreType.DMA,
            ],
        )

    ready_one = plan[1][-1]
    ready_two = plan[2][-1]
    image = merged((0, 1), [(1, ready_one - 1)], False, None)
    image = merged(
        (0, 1, 2), [(tiles - 1, 1), (0, 1), (ready_one, ready_two - ready_one)], True, image
    )
    return merged((0, 1, 2, 3), [(ready_two, tiles - 1 - ready_two)], False, image)


def solution(mesh):
    return jax.shard_map(
        body,
        mesh=mesh,
        in_specs=(P("aper", None, "rng", "beam"),) + (P(),) * 12,
        out_specs=P("aper", None, "rng", "beam"),
        check_vma=False,
    )
```

profile of v0, /device:TPU:0, one launch (start us, length us, event | category | flops | bytes accessed | tf_op | source)
XLA Modules:
  0.0 66.6 jit_solution(4935108451156039738)
XLA Ops:
  0.0 0.1 pad_add_fusion.sc
  0.1 1.8 %shard_map.127 = (f32[2,32,512]{2,1,0:T(8,128)S(1)}, f32[2,32,512]{2,1,0:T(8,128)S(1)}, f32[2,32,512]{2,1,0:T(8,128)S(1)}) custom-call(s32[4]{0:T(128)S(1)} %pad_add_fusion.sc, f32[1,2,2048,128]{3,2,1,0:T(8,128)} %child.3), custom_call_target="tpu_custom_call" | custom-call | tf_op jit(solution)/shard_map/pallas_call | solution.py:497
  1.9 2.7 %shard_map.128 = (f32[2,8,2048]{2,1,0:T(8,128)S(1)}, f32[2,128,2048]{2,1,0:T(8,128)S(1)}) custom-call(s32[4]{0:T(128)S(1)} %pad_add_fusion.sc, f32[1,2,2048,128]{3,2,1,0:T(8,128)} %child.3, f32[2,32,512]{2,1,0:T(8,128)S(1)} %get-tuple-element.31.after), custom_call_target="tpu_custom_call" | custom-call | tf_op jit(solution)/shard_map/pallas_call | solution.py:497
  4.6 0.6 collective-permute-start
  5.2 1.0 %collective-permute-done.rim = f32[2,8,2048]{2,1,0:T(8,128)S(1)} collective-permute-done((f32[2,8,2048]{2,1,0:T(8,128)S(1)}, f32[2,8,2048]{2,1,0:T(8,128)S(1)}, u32[]{:S(2)}, u32[]{:S(2)}) %collective-permute-start) | collective-permute-done | bytes 131104 | tf_op jit(solution)/shard_map/ppermute | solution.py:525
  6.2 0.0 copy-start.5
  6.2 0.0 copy-start.7
  6.2 0.0 copy-start.8
  6.2 0.0 copy-start.11
  6.3 0.9 %shard_map.129 = (f32[2,64,512]{2,1,0:T(8,128)S(1)}, f32[2,64,512]{2,1,0:T(8,128)S(1)}, f32[2,64,512]{2,1,0:T(8,128)S(1)}, f32[2,48,512]{2,1,0:T(8,128)S(1)}, f3...) custom-call(s32[4]{0:T(128)S(1)} %pad_add_fusion.sc, ...), custom_call_target="tpu_custom_call" | custom-call | tf_op jit(solution)/shard_map/pallas_call | solution.py:497
  7.1 2.9 %collective-permute-start.4 = (f32[2,64,512]{2,1,0:T(8,128)S(1)}, f32[2,64,512]{2,1,0:T(8,128)S(1)}, u32[]{:S(2)}, u32[]{:S(2)}) collective-permute-start(f32[2,64,512]{2,1,0:T(8,128)S(1)} %get-tuple-element.37), channel_id=1, source_target_pairs={{0,8},{8,0},{16,24},{24,16},{1,9},{9,1},{17,25},{25,17},{2,10},{10... | collective-permute-start | bytes 786440 | tf_op jit(solution)/shard_map/ppermute | solution.py:500
  10.0 1.5 %collective-permute-start.2 = (f32[2,32,512]{2,1,0:T(8,128)S(1)}, f32[2,32,512]{2,1,0:T(8,128)S(1)}, u32[]{:S(2)}, u32[]{:S(2)}) collective-permute-start(f32[2,32,512]{2,1,0:T(8,128)S(1)} %get-tuple-element.35), channel_id=1, source_target_pairs={{0,16},{8,24},{16,0},{24,8},{1,17},{9,25},{17,1},{25,9},{2,18},{10... | collective-permute-start | bytes 393224 | tf_op jit(solution)/shard_map/ppermute | solution.py:500
  11.6 0.0 collective-permute-start.3
  11.6 1.9 %collective-permute-start.1 = (f32[2,32,512]{2,1,0:T(8,128)S(1)}, f32[2,32,512]{2,1,0:T(8,128)S(1)}, u32[]{:S(2)}, u32[]{:S(2)}) collective-permute-start(f32[2,32,512]{2,1,0:T(8,128)S(1)} %get-tuple-element.31.after), channel_id=1, source_target_pairs={{0,8},{8,0},{16,24},{24,16},{1,9},{9,1},{17,25},{25,17},{2,10},{10... | collective-permute-start | bytes 393224 | tf_op jit(solution)/shard_map/ppermute | solution.py:500
  13.5 1.5 %collective-permute-start.5 = (f32[2,64,512]{2,1,0:T(8,128)S(1)}, f32[2,64,512]{2,1,0:T(8,128)S(1)}, u32[]{:S(2)}, u32[]{:S(2)}) collective-permute-start(f32[2,64,512]{2,1,0:T(8,128)S(1)} %get-tuple-element.38), channel_id=1, source_target_pairs={{0,16},{8,24},{16,0},{24,8},{1,17},{9,25},{17,1},{25,9},{2,18},{10... | collective-permute-start | bytes 786440 | tf_op jit(solution)/shard_map/ppermute | solution.py:500
  15.1 0.4 collective-permute-done.2.refs_1_.refs_2_.refs_4_
  15.5 1.5 %collective-permute-start.6 = (f32[2,64,512]{2,1,0:T(8,128)S(1)}, f32[2,64,512]{2,1,0:T(8,128)S(1)}, u32[]{:S(2)}, u32[]{:S(2)}) collective-permute-start(f32[2,64,512]{2,1,0:T(8,128)S(1)} %get-tuple-element.39), channel_id=1, source_target_pairs={{0,24},{8,16},{16,8},{24,0},{1,25},{9,17},{17,9},{25,1},{2,26},{10... | collective-permute-start | bytes 786440 | tf_op jit(solution)/shard_map/ppermute | solution.py:500
  17.0 4.6 %collective-permute-done.3.refs_2_.refs_3_.refs_5_ = f32[2,32,512]{2,1,0:T(8,128)S(1)} collective-permute-done((f32[2,32,512]{2,1,0:T(8,128)S(1)}, f32[2,32,512]{2,1,0:T(8,128)S(1)}, u32[]{:S(2)}, u32[]{:S(2)}) %collective-permute-start.3) | collective-permute-done | bytes 131104 | tf_op jit(solution)/shard_map/ppermute | solution.py:500
  21.5 1.5 %collective-permute-start.7 = (f32[2,48,512]{2,1,0:T(8,128)S(1)}, f32[2,48,512]{2,1,0:T(8,128)S(1)}, u32[]{:S(2)}, u32[]{:S(2)}) collective-permute-start(f32[2,48,512]{2,1,0:T(8,128)S(1)} %get-tuple-element.40), channel_id=1, source_target_pairs={{0,8},{8,0},{16,24},{24,16},{1,9},{9,1},{17,25},{25,17},{2,10},{10... | collective-permute-start | bytes 589832 | tf_op jit(solution)/shard_map/ppermute | solution.py:500
  23.0 1.9 %collective-permute-start.8 = (f32[2,48,512]{2,1,0:T(8,128)S(1)}, f32[2,48,512]{2,1,0:T(8,128)S(1)}, u32[]{:S(2)}, u32[]{:S(2)}) collective-permute-start(f32[2,48,512]{2,1,0:T(8,128)S(1)} %get-tuple-element.41), channel_id=1, source_target_pairs={{0,16},{8,24},{16,0},{24,8},{1,17},{9,25},{17,1},{25,9},{2,18},{10... | collective-permute-start | bytes 589832 | tf_op jit(solution)/shard_map/ppermute | solution.py:500
  24.9 1.4 %collective-permute-start.9 = (f32[2,48,512]{2,1,0:T(8,128)S(1)}, f32[2,48,512]{2,1,0:T(8,128)S(1)}, u32[]{:S(2)}, u32[]{:S(2)}) collective-permute-start(f32[2,48,512]{2,1,0:T(8,128)S(1)} %get-tuple-element.42), channel_id=1, source_target_pairs={{0,24},{8,16},{16,8},{24,0},{1,25},{9,17},{17,9},{25,1},{2,26},{10... | collective-permute-start | bytes 589832 | tf_op jit(solution)/shard_map/ppermute | solution.py:500
  26.4 3.3 %collective-permute-done.5.refs_4_.refs_5_.refs_7_ = f32[2,64,512]{2,1,0:T(8,128)S(1)} collective-permute-done((f32[2,64,512]{2,1,0:T(8,128)S(1)}, f32[2,64,512]{2,1,0:T(8,128)S(1)}, u32[]{:S(2)}, u32[]{:S(2)}) %collective-permute-start.5) | collective-permute-done | bytes 262176 | tf_op jit(solution)/shard_map/ppermute | solution.py:500
  29.7 0.4 collective-permute-done.6.refs_5_.refs_6_.refs_8_
  30.1 3.5 %collective-permute-start.13 = (f32[4,2,48,128]{3,2,1,0:T(8,128)S(1)}, f32[4,2,48,128]{3,2,1,0:T(8,128)S(1)}, u32[]{:S(2)}, u32[]{:S(2)}) collective-permute-start(f32[4,2,48,128]{3,2,1,0:T(8,128)S(1)} %get-tuple-element.55), channel_id=1, source_target_pairs={{0,2},{2,4},{4,6},{1,3},{3,5},{5,7},{8,10},{10,12},{12,14},{9,11},... | collective-permute-start | bytes 589832 | tf_op jit(solution)/shard_map/ppermute | solution.py:548
  33.6 1.3 %collective-permute-start.14 = (f32[4,2,48,128]{3,2,1,0:T(8,128)S(1)}, f32[4,2,48,128]{3,2,1,0:T(8,128)S(1)}, u32[]{:S(2)}, u32[]{:S(2)}) collective-permute-start(f32[4,2,48,128]{3,2,1,0:T(8,128)S(1)} %get-tuple-element.56), channel_id=1, source_target_pairs={{2,0},{4,2},{6,4},{3,1},{5,3},{7,5},{10,8},{12,10},{14,12},{11,9},... | collective-permute-start | bytes 589832 | tf_op jit(solution)/shard_map/ppermute | solution.py:549
  34.9 2.2 %collective-permute-done.8.refs_10_.refs_8_ = f32[2,48,512]{2,1,0:T(8,128)S(1)} collective-permute-done((f32[2,48,512]{2,1,0:T(8,128)S(1)}, f32[2,48,512]{2,1,0:T(8,128)S(1)}, u32[]{:S(2)}, u32[]{:S(2)}) %collective-permute-start.8) | collective-permute-done | bytes 196640 | tf_op jit(solution)/shard_map/ppermute | solution.py:500
  37.1 2.2 %collective-permute-start.11 = (f32[2,48,512]{2,1,0:T(8,128)S(1)}, f32[2,48,512]{2,1,0:T(8,128)S(1)}, u32[]{:S(2)}, u32[]{:S(2)}) collective-permute-start(f32[2,48,512]{2,1,0:T(8,128)S(1)} %get-tuple-element.44), channel_id=1, source_target_pairs={{0,16},{8,24},{16,0},{24,8},{1,17},{9,25},{17,1},{25,9},{2,18},{10... | collective-permute-start | bytes 589832 | tf_op jit(solution)/shard_map/ppermute | solution.py:500
  39.3 0.6 collective-permute-start.12
  40.0 1.4 %shard_map.130 = (f32[2,16,128]{2,1,0:T(8,128)S(1)}, bf16[2,256,256]{2,1,0:T(8,128)(2,1)S(1)}, bf16[2,128,256]{2,1,0:T(8,128)(2,1)S(1)}, f32[2,2,24,128]{3,2,1,0...) custom-call(s32[4]{0:T(128)S(1)} %pad_add_fusion.sc, ...), custom_call_target="tpu_custom_call" | custom-call | tf_op jit(solution)/shard_map/pallas_call | solution.py:497
  41.4 6.8 %shard_map.132.refs_21_ = f32[1,2,2048,128]{3,2,1,0:T(8,128)} custom-call(s32[4]{0:T(128)S(1)} %pad_add_fusion.sc, f32[2,48,2048]{2,1,0:T(8,128)S(1)} %get-tuple-element.34.own.refs_0_, f32[2,32,512]{2,1,0:T(8,128)S(1)} %collective-permute-done.1.refs_0_.refs_1_.refs_3_, f32[2,32,512]{2,1,0:T(8,128)S(1)} %collective-permute-done.2.refs_1_.refs_2_.refs_4_, ...), custom_call_target="tpu_custom_call" | custom-call | tf_op jit(solution)/shard_map/pallas_call | solution.py:497
  48.3 8.9 %shard_map.133.refs_22_ = f32[1,2,2048,128]{3,2,1,0:T(8,128)} custom-call(s32[4]{0:T(128)S(1)} %pad_add_fusion.sc, f32[2,48,2048]{2,1,0:T(8,128)S(1)} %get-tuple-element.34.own.refs_0_, f32[4,2,48,128]{3,2,1,0:T(8,128)S(1)} %collective-permute-done.13.refs_1_, ...), custom_call_target="tpu_custom_call", output_to_operand_aliasing={{}: (22, {})} | custom-call | tf_op jit(solution)/shard_map/pallas_call | solution.py:497
  57.2 9.4 %shard_map.134 = f32[1,2,2048,128]{3,2,1,0:T(8,128)} custom-call(s32[4]{0:T(128)S(1)} %pad_add_fusion.sc, f32[2,48,2048]{2,1,0:T(8,128)S(1)} %get-tuple-element.34.own.refs_0_, f32[2,32,512]{2,1,0:T(8,128)S(1)} %collective-permute-done.1.refs_0_.refs_1_.refs_3_, ...), custom_call_target="tpu_custom_call", output_to_operand_aliasing={{}: (23, {})} | custom-call | tf_op jit(solution)/shard_map/pallas_call | solution.py:497
  (31 shorter events, 0.1 us)
Async XLA Ops:
  4.6 1.5 %collective-permute-start = (f32[2,8,2048]{2,1,0:T(8,128)S(1)}, f32[2,8,2048]{2,1,0:T(8,128)S(1)}, u32[]{:S(2)}, u32[]{:S(2)}) collective-permute-start(f32[2,8,2048]{2,1,0:T(8,128)S(1)} %get-tuple-element.33), channel_id=1, source_target_pairs={{0,1},{1,0},{2,3},{3,2},{4,5},{5,4},{6,7},{7,6},{8,9},{9,8},{10,11... | collective-permute-start | bytes 393224 | tf_op jit(solution)/shard_map/ppermute | solution.py:525
  6.2 33.8 %copy-start = (f32[2,8,1024]{2,1,0:T(8,128)S(1)}, f32[2,8,1024]{2,1,0:T(8,128)}, u32[]{:S(2)}) copy-start(f32[2,8,1024]{2,1,0:T(8,128)} %btaps_two.1) | copy-start | bytes 196612
  6.2 33.8 %copy-start.1 = (f32[2,8,512]{2,1,0:T(8,128)S(1)}, f32[2,8,512]{2,1,0:T(8,128)}, u32[]{:S(2)}) copy-start(f32[2,8,512]{2,1,0:T(8,128)} %btaps_one.1) | copy-start | bytes 98308
  6.2 33.8 %copy-start.2 = (f32[2,8,512]{2,1,0:T(8,128)S(1)}, f32[2,8,512]{2,1,0:T(8,128)}, u32[]{:S(2)}) copy-start(f32[2,8,512]{2,1,0:T(8,128)} %rtaps_two.1) | copy-start | bytes 98308
  6.2 33.8 %copy-start.3 = (f32[2,8,256]{2,1,0:T(8,128)S(1)}, f32[2,8,256]{2,1,0:T(8,128)}, u32[]{:S(2)}) copy-start(f32[2,8,256]{2,1,0:T(8,128)} %rtaps_one.1) | copy-start | bytes 49156
  6.2 33.8 %copy-start.4 = (s32[2,1024]{1,0:T(2,128)S(1)}, s32[2,1024]{1,0:T(2,128)}, u32[]{:S(2)}) copy-start(s32[2,1024]{1,0:T(2,128)} %bstart_two.1) | copy-start | bytes 24580
  6.2 33.8 %copy-start.5 = (f32[2,1024]{1,0:T(2,128)S(1)}, f32[2,1024]{1,0:T(2,128)}, u32[]{:S(2)}) copy-start(f32[2,1024]{1,0:T(2,128)} %prate_two.1) | copy-start | bytes 24580
  6.2 33.8 %copy-start.6 = (f32[2,1024]{1,0:T(2,128)S(1)}, f32[2,1024]{1,0:T(2,128)}, u32[]{:S(2)}) copy-start(f32[2,1024]{1,0:T(2,128)} %poff_two.1) | copy-start | bytes 24580
  6.2 33.8 %copy-start.7 = (s32[2,512]{1,0:T(2,128)S(1)}, s32[2,512]{1,0:T(2,128)}, u32[]{:S(2)}) copy-start(s32[2,512]{1,0:T(2,128)} %bstart_one.1) | copy-start | bytes 12292
  6.2 33.8 %copy-start.8 = (f32[2,512]{1,0:T(2,128)S(1)}, f32[2,512]{1,0:T(2,128)}, u32[]{:S(2)}) copy-start(f32[2,512]{1,0:T(2,128)} %prate_one.1) | copy-start | bytes 12292
  6.2 33.8 %copy-start.9 = (f32[2,512]{1,0:T(2,128)S(1)}, f32[2,512]{1,0:T(2,128)}, u32[]{:S(2)}) copy-start(f32[2,512]{1,0:T(2,128)} %poff_one.1) | copy-start | bytes 12292
  6.2 33.8 %copy-start.10 = (s32[2,512]{1,0:T(2,128)S(1)}, s32[2,512]{1,0:T(2,128)}, u32[]{:S(2)}) copy-start(s32[2,512]{1,0:T(2,128)} %shift_two.1) | copy-start | bytes 12292
  6.2 33.8 %copy-start.11 = (s32[2,256]{1,0:T(2,128)S(1)}, s32[2,256]{1,0:T(2,128)}, u32[]{:S(2)}) copy-start(s32[2,256]{1,0:T(2,128)} %shift_one.1) | copy-start | bytes 6148
  7.1 17.8 %collective-permute-start.4 = (f32[2,64,512]{2,1,0:T(8,128)S(1)}, f32[2,64,512]{2,1,0:T(8,128)S(1)}, u32[]{:S(2)}, u32[]{:S(2)}) collective-permute-start(f32[2,64,512]{2,1,0:T(8,128)S(1)} %get-tuple-element.37), channel_id=1, source_target_pairs={{0,8},{8,0},{16,24},{24,16},{1,9},{9,1},{17,25},{25,17},{2,10},{10... | collective-permute-start | bytes 786440 | tf_op jit(solution)/shard_map/ppermute | solution.py:500
  10.0 5.4 %collective-permute-start.2 = (f32[2,32,512]{2,1,0:T(8,128)S(1)}, f32[2,32,512]{2,1,0:T(8,128)S(1)}, u32[]{:S(2)}, u32[]{:S(2)}) collective-permute-start(f32[2,32,512]{2,1,0:T(8,128)S(1)} %get-tuple-element.35), channel_id=1, source_target_pairs={{0,16},{8,24},{16,0},{24,8},{1,17},{9,25},{17,1},{25,9},{2,18},{10... | collective-permute-start | bytes 393224 | tf_op jit(solution)/shard_map/ppermute | solution.py:500
  11.6 10.0 %collective-permute-start.3 = (f32[2,32,512]{2,1,0:T(8,128)S(1)}, f32[2,32,512]{2,1,0:T(8,128)S(1)}, u32[]{:S(2)}, u32[]{:S(2)}) collective-permute-start(f32[2,32,512]{2,1,0:T(8,128)S(1)} %get-tuple-element.36), channel_id=1, source_target_pairs={{0,24},{8,16},{16,8},{24,0},{1,25},{9,17},{17,9},{25,1},{2,26},{10... | collective-permute-start | bytes 393224 | tf_op jit(solution)/shard_map/ppermute | solution.py:500
  11.6 11.5 %collective-permute-start.1 = (f32[2,32,512]{2,1,0:T(8,128)S(1)}, f32[2,32,512]{2,1,0:T(8,128)S(1)}, u32[]{:S(2)}, u32[]{:S(2)}) collective-permute-start(f32[2,32,512]{2,1,0:T(8,128)S(1)} %get-tuple-element.31.after), channel_id=1, source_target_pairs={{0,8},{8,0},{16,24},{24,16},{1,9},{9,1},{17,25},{25,17},{2,10},{10... | collective-permute-start | bytes 393224 | tf_op jit(solution)/shard_map/ppermute | solution.py:500
  13.5 16.1 %collective-permute-start.5 = (f32[2,64,512]{2,1,0:T(8,128)S(1)}, f32[2,64,512]{2,1,0:T(8,128)S(1)}, u32[]{:S(2)}, u32[]{:S(2)}) collective-permute-start(f32[2,64,512]{2,1,0:T(8,128)S(1)} %get-tuple-element.38), channel_id=1, source_target_pairs={{0,16},{8,24},{16,0},{24,8},{1,17},{9,25},{17,1},{25,9},{2,18},{10... | collective-permute-start | bytes 786440 | tf_op jit(solution)/shard_map/ppermute | solution.py:500
  15.5 14.6 %collective-permute-start.6 = (f32[2,64,512]{2,1,0:T(8,128)S(1)}, f32[2,64,512]{2,1,0:T(8,128)S(1)}, u32[]{:S(2)}, u32[]{:S(2)}) collective-permute-start(f32[2,64,512]{2,1,0:T(8,128)S(1)} %get-tuple-element.39), channel_id=1, source_target_pairs={{0,24},{8,16},{16,8},{24,0},{1,25},{9,17},{17,9},{25,1},{2,26},{10... | collective-permute-start | bytes 786440 | tf_op jit(solution)/shard_map/ppermute | solution.py:500
  21.5 12.0 %collective-permute-start.7 = (f32[2,48,512]{2,1,0:T(8,128)S(1)}, f32[2,48,512]{2,1,0:T(8,128)S(1)}, u32[]{:S(2)}, u32[]{:S(2)}) collective-permute-start(f32[2,48,512]{2,1,0:T(8,128)S(1)} %get-tuple-element.40), channel_id=1, source_target_pairs={{0,8},{8,0},{16,24},{24,16},{1,9},{9,1},{17,25},{25,17},{2,10},{10... | collective-permute-start | bytes 589832 | tf_op jit(solution)/shard_map/ppermute | solution.py:500
  23.0 14.0 %collective-permute-start.8 = (f32[2,48,512]{2,1,0:T(8,128)S(1)}, f32[2,48,512]{2,1,0:T(8,128)S(1)}, u32[]{:S(2)}, u32[]{:S(2)}) collective-permute-start(f32[2,48,512]{2,1,0:T(8,128)S(1)} %get-tuple-element.41), channel_id=1, source_target_pairs={{0,16},{8,24},{16,0},{24,8},{1,17},{9,25},{17,1},{25,9},{2,18},{10... | collective-permute-start | bytes 589832 | tf_op jit(solution)/shard_map/ppermute | solution.py:500
  24.9 14.4 %collective-permute-start.9 = (f32[2,48,512]{2,1,0:T(8,128)S(1)}, f32[2,48,512]{2,1,0:T(8,128)S(1)}, u32[]{:S(2)}, u32[]{:S(2)}) collective-permute-start(f32[2,48,512]{2,1,0:T(8,128)S(1)} %get-tuple-element.42), channel_id=1, source_target_pairs={{0,24},{8,16},{16,8},{24,0},{1,25},{9,17},{17,9},{25,1},{2,26},{10... | collective-permute-start | bytes 589832 | tf_op jit(solution)/shard_map/ppermute | solution.py:500
  29.7 27.6 %collective-permute-start.10 = (f32[2,48,512]{2,1,0:T(8,128)S(1)}, f32[2,48,512]{2,1,0:T(8,128)S(1)}, u32[]{:S(2)}, u32[]{:S(2)}) collective-permute-start(f32[2,48,512]{2,1,0:T(8,128)S(1)} %get-tuple-element.43), channel_id=1, source_target_pairs={{0,8},{8,0},{16,24},{24,16},{1,9},{9,1},{17,25},{25,17},{2,10},{10... | collective-permute-start | bytes 589832 | tf_op jit(solution)/shard_map/ppermute | solution.py:500
  30.1 18.2 %collective-permute-start.13 = (f32[4,2,48,128]{3,2,1,0:T(8,128)S(1)}, f32[4,2,48,128]{3,2,1,0:T(8,128)S(1)}, u32[]{:S(2)}, u32[]{:S(2)}) collective-permute-start(f32[4,2,48,128]{3,2,1,0:T(8,128)S(1)} %get-tuple-element.55), channel_id=1, source_target_pairs={{0,2},{2,4},{4,6},{1,3},{3,5},{5,7},{8,10},{10,12},{12,14},{9,11},... | collective-permute-start | bytes 589832 | tf_op jit(solution)/shard_map/ppermute | solution.py:548
  33.6 14.7 %collective-permute-start.14 = (f32[4,2,48,128]{3,2,1,0:T(8,128)S(1)}, f32[4,2,48,128]{3,2,1,0:T(8,128)S(1)}, u32[]{:S(2)}, u32[]{:S(2)}) collective-permute-start(f32[4,2,48,128]{3,2,1,0:T(8,128)S(1)} %get-tuple-element.56), channel_id=1, source_target_pairs={{2,0},{4,2},{6,4},{3,1},{5,3},{7,5},{10,8},{12,10},{14,12},{11,9},... | collective-permute-start | bytes 589832 | tf_op jit(solution)/shard_map/ppermute | solution.py:549
  37.1 20.2 %collective-permute-start.11 = (f32[2,48,512]{2,1,0:T(8,128)S(1)}, f32[2,48,512]{2,1,0:T(8,128)S(1)}, u32[]{:S(2)}, u32[]{:S(2)}) collective-permute-start(f32[2,48,512]{2,1,0:T(8,128)S(1)} %get-tuple-element.44), channel_id=1, source_target_pairs={{0,16},{8,24},{16,0},{24,8},{1,17},{9,25},{17,1},{25,9},{2,18},{10... | collective-permute-start | bytes 589832 | tf_op jit(solution)/shard_map/ppermute | solution.py:500
  39.3 17.9 %collective-permute-start.12 = (f32[2,48,512]{2,1,0:T(8,128)S(1)}, f32[2,48,512]{2,1,0:T(8,128)S(1)}, u32[]{:S(2)}, u32[]{:S(2)}) collective-permute-start(f32[2,48,512]{2,1,0:T(8,128)S(1)} %get-tuple-element.45), channel_id=1, source_target_pairs={{0,24},{8,16},{16,8},{24,0},{1,25},{9,17},{17,9},{25,1},{2,26},{10... | collective-permute-start | bytes 589832 | tf_op jit(solution)/shard_map/ppermute | solution.py:500
where the time goes:
time: 66.8 us; the launch traced here: 66.6 us
  Pallas kernels  31.9 us (48%)
  starting transfers between devices  22.4 us (34%)
  waiting for transfers between devices  11.9 us (18%)
    pallas_call x8, Pallas kernels, call(): return pl.pallas_call(kernel, compiler_params=PARAMS, **settings)(*operands)  31.9 us
    ppermute x12, starting transfers between devices, swap(): return lax.ppermute(block, 'aper', [(i, i ^ k) for i in range(apers)])  17.1 us
    ppermute x12, waiting for transfers between devices, swap(): return lax.ppermute(block, 'aper', [(i, i ^ k) for i in range(apers)])  10.9 us
    ppermute x1, starting transfers between devices, body(): low = lax.ppermute(to_high, 'rng', [(i, i + 1) for i in range(ranks - 1)])  3.49 us
  transfers between devices with their start and end apart: 15, of which 6 were waited for; matrix products, arithmetic and copies ran while one was open for 0% of the time, Pallas kernels for 26%

commit v1 on v0

--- a/solution.py
+++ b/solution.py
@@ -15,7 +15,8 @@
 RIM = 8
 PRIM = 5
 HALO = 16
-FINE = 2 * TAPS - 1
+COARSE = 4
+FINE = TAPS + COARSE - 1
 ANY = pl.BlockSpec(memory_space=pl.ANY)
 HBM = pl.BlockSpec(memory_space=pltpu.HBM)
 SMEM = pl.BlockSpec(memory_space=pltpu.SMEM)
@@ -52,44 +53,32 @@
 
 
 def first_pack(plan, sc, child, *refs):
-    outs, (rows_in, turned, sem) = refs[:3], refs[3:]
-    sub = child.shape[3] // GROUP
-    runs = spans(plan[0])
-    copies = [fetch(child, rows_in, first, count, sem) for _, first, count in runs]
-    for copy in copies:
-        copy.start()
-    for copy in copies:
-        copy.wait()
-    for position, tile in enumerate(plan[0]):
-        for part in range(2):
-            turned[part, :, lanes(position)] = rows_in[part, lanes(tile), :].T
-    for k in range(1, GROUP):
-        start = pl.multiple_of(jnp.bitwise_xor(sc[0], k) * sub, 8)
-        for part in range(2):
-            outs[k - 1][part] = turned[part, pl.ds(start, sub), :]
-
-
-def turn_all(sc, child, after, rim, turned, rows_in, sems):
-    del after
+    outs, (rim, turned, rows_in, sems) = refs[:3], refs[3:]
     blk = child.shape[3]
-    tiles = child.shape[2] // TILE
-    step = tiles // 4
-    copies = [fetch(child, rows_in, i * step, step, sems.at[i]) for i in range(4)]
-    for copy in copies:
-        copy.start()
-    for i, copy in enumerate(copies):
-        copy.wait()
-
-        def turn(j, carry):
-            tile = i * step + j
+    sub = blk // GROUP
+    parts = [spans(part) for part in plan]
+    copies = [
+        [fetch(child, rows_in, first, count, sems.at[i]) for _, first, count in part]
+        for i, part in enumerate(parts)
+    ]
+    for part in copies:
+        for copy in part:
+            copy.start()
+    for i, part in enumerate(copies):
+        for copy in part:
+            copy.wait()
+        for tile in plan[i]:
             for part in range(2):
                 turned[part, :, lanes(tile)] = rows_in[part, lanes(tile), :].T
-            return carry
-
-        lax.fori_loop(0, step, turn, 0, unroll=2)
+        if i == 0:
+            for k in range(1, GROUP):
+                start = pl.multiple_of(jnp.bitwise_xor(sc[0], k) * sub, 8)
+                for position, first, count in parts[0]:
+                    outs[k - 1][:, :, lanes(position, count)] = turned[
+                        :, pl.ds(start, sub), lanes(first, count)
+                    ]
     side = pl.multiple_of((1 - sc[1]) * (blk - RIM), 8)
-    for part in range(2):
-        rim[part] = turned[part, pl.ds(side, RIM), :]
+    rim[...] = turned[:, pl.ds(side, RIM), :]
 
 
 def second_pack(plan, sc, turned, rim, *refs):
@@ -156,13 +145,15 @@
 
 def spread(load, store_to, rows, table):
     coarse = table[FINE : FINE + 1, :]
-    near, far = coarse == 1.0, coarse == 2.0
+    options = 2 * SPAN // COARSE + 1
+    chosen = [coarse == float(i) for i in range(1, options)]
     step = 64
     for start in range(0, rows, step):
         size = min(step, rows - start)
-        store_to[pl.ds(start, size), :] = jnp.where(
-            far, load(start + 16, size), jnp.where(near, load(start + 8, size), load(start, size))
-        )
+        value = load(start, size)
+        for i in range(1, options):
+            value = jnp.where(chosen[i - 1], load(start + i * COARSE, size), value)
+        store_to[pl.ds(start, size), :] = value
 
 
 def fine_taps(shifted, start, size, table):
@@ -201,7 +192,7 @@
     del refs[:9]
     if keep:
         refs.pop(0)
-    out, flat, shifted, lhs, mixed, parent, done, out_sem = refs
+    out, flat, shifted, shifted_two, lhs, lhs_two, mixed, mixed_two, parent, done, out_sem = refs
     tiles = own.shape[2] // TILE
     row_base, rows_total = sc[2], sc[3]
     wide = sub + 2 * RIM
@@ -227,11 +218,10 @@
                 for part in range(2):
 
                     def load(start, size):
-                        return flat[
-                            side, part, pl.ds(pl.multiple_of(i * TILE + TILE - 2 * HALO + start, 8), size), :
-                        ]
-
-                    spread(load, shifted.at[side, part], rows + 24, taps_one[side])
+                        base = pl.multiple_of(i * TILE + TILE - 2 * HALO, 8)
+                        return flat[side, part, pl.ds(base + start, size), :]
+
+                    spread(load, shifted.at[side, part], rows + 16, taps_one[side])
                     for start in range(0, rows, min(rows, half)):
                         size = min(rows, half)
                         split_into(
@@ -274,38 +264,30 @@
                             image
                         ][part]
 
-        def full_block(i, carry):
-            parent_block(i, TILE)
-            return carry
-
-        lax.fori_loop(0, count, full_block, 0)
-        parent_block(count, 2 * HALO)
-        parent[:, :, pl.ds(count * TILE + 2 * HALO, 16), :] = jnp.zeros((2, 2, 16, TILE), F32)
-
-        def final_block(i, carry):
+        def final_block(i):
             for image in range(2):
                 for part in range(2):
 
                     def load(start, size):
-                        return parent[image, part, pl.ds(pl.multiple_of(i * TILE + start, 8), size), :]
-
-                    spread(load, shifted.at[image, part], TILE + 24, taps_two[image])
+                        return parent[image, part, pl.ds(pl.multiple_of(i * TILE, 8) + start, size), :]
+
+                    spread(load, shifted_two.at[image, part], TILE + 16, taps_two[image])
                     for start in range(0, TILE, half):
                         split_into(
-                            lhs.at[image],
+                            lhs_two.at[image],
                             part * TILE + start,
                             half,
-                            fine_taps(shifted.at[image, part], start, half, taps_two[image]),
+                            fine_taps(shifted_two.at[image, part], start, half, taps_two[image]),
                         )
-                mixed[image] = jnp.dot(lhs[image], mats_two[image], preferred_element_type=F32)
+                mixed_two[image] = jnp.dot(lhs_two[image], mats_two[image], preferred_element_type=F32)
             size = 32
             for start in range(0, TILE, size):
                 sums = [None, None]
                 for image in range(2):
                     cosine, sine = turn_factor(base_two, fine_two, image, first + i, start, size)
                     real, imag = (
-                        mixed[image, pl.ds(part * TILE + start, size), pl.ds(0, TILE)]
-                        + mixed[image, pl.ds(part * TILE + start, size), pl.ds(TILE, TILE)]
+                        mixed_two[image, pl.ds(part * TILE + start, size), pl.ds(0, TILE)]
+                        + mixed_two[image, pl.ds(part * TILE + start, size), pl.ds(TILE, TILE)]
                         for part in range(2)
                     )
                     terms = (cosine * real - sine * imag, sine * real + cosine * imag)
@@ -313,9 +295,21 @@
                         sums[part] = terms[part] if sums[part] is None else sums[part] + terms[part]
                 for part in range(2):
                     done[part, pl.ds(pl.multiple_of((done_at + i) * TILE + start, 8), size), :] = sums[part]
-            return carry
-
-        lax.fori_loop(0, count, final_block, 0)
+
+        parent_block(0, TILE)
+        if count > 1:
+            parent_block(1, TILE)
+
+            def both(i, carry):
+                final_block(i)
+                parent_block(i + 2, TILE)
+                return carry
+
+            if count > 2:
+                lax.fori_loop(0, count - 2, both, 0)
+            final_block(count - 2)
+        parent_block(count, 2 * HALO)
+        final_block(count - 1)
         result = pltpu.make_async_copy(
             done.at[:, lanes(done_at, count), :], out.at[0, :, lanes(first, count), :], out_sem
         )
@@ -375,11 +369,11 @@
     def range_table(target, shifts, taps):
         moved = shifts[0:1, :] + SPAN
         spot = lax.broadcasted_iota(jnp.int32, (2 * TAPS, TILE), 0)
-        apart = spot - lax.rem(moved, jnp.int32(TAPS))
+        apart = spot - lax.rem(moved, jnp.int32(COARSE))
         total_rows = jnp.zeros((2 * TAPS, TILE), F32)
         for k in range(TAPS):
             total_rows = total_rows + jnp.where(apart == k, taps[k : k + 1, :], 0.0)
-        target[...] = jnp.where(spot == FINE, (moved // TAPS).astype(F32), total_rows)
+        target[...] = jnp.where(spot == FINE, (moved // COARSE).astype(F32), total_rows)
 
     def beam_matrix(starts, taps, first, height):
         apart = lax.broadcasted_iota(jnp.int32, (height, TILE), 0) - (starts[0:1, :] - first)
@@ -501,27 +495,16 @@
 
     children = pltpu.with_memory_space_constraint(children, pltpu.HBM)
     widths = [len(part) * TILE for part in plan]
-    edge = call(
+    *edge, rim, turned = call(
         functools.partial(first_pack, plan),
-        sc, children,
-        out_shape=[out(2, sub, widths[0])] * 3,
+        sc,
+        children,
+        out_shape=[out(2, sub, widths[0])] * 3 + [out(2, RIM, rows), out(2, blk, rows)],
         in_specs=[SMEM, HBM],
-        out_specs=[VMEM] * 3,
-        scratch_shapes=[
-            pltpu.VMEM((2, rows, blk), F32),
-            pltpu.VMEM((2, blk, widths[0]), F32),
-            pltpu.SemaphoreType.DMA,
-        ],
+        out_specs=[VMEM] * 5,
+        scratch_shapes=[pltpu.VMEM((2, rows, blk), F32), pltpu.SemaphoreType.DMA((4,))],
     )
     remote = {0: [swap(edge[k - 1], k) for k in range(1, GROUP)]}
-    rim, turned = call(
-        turn_all,
-        sc, children, edge[0],
-        out_shape=[out(2, RIM, rows), out(2, blk, rows)],
-        in_specs=[SMEM, HBM, ANY],
-        out_specs=[VMEM] * 2,
-        scratch_shapes=[pltpu.VMEM((2, rows, blk), F32), pltpu.SemaphoreType.DMA((4,))],
-    )
     rim = lax.ppermute(rim, "beam", [(0, 1), (1, 0)])
     *packed, own = call(
         functools.partial(second_pack, plan),
@@ -600,10 +583,10 @@
             input_output_aliases={len(operands) - 1: 0} if keep else {},
             scratch_shapes=[
                 pltpu.VMEM((2, 2, (longest + 2) * TILE, TILE), F32),
-                pltpu.VMEM((2, 2, TILE + 24, TILE), F32),
-                pltpu.VMEM((2, 2 * TILE, 2 * TILE), BF16),
-                pltpu.VMEM((2, 2 * TILE, 2 * TILE), F32),
-                pltpu.VMEM((2, 2, longest * TILE + 2 * HALO + 16, TILE), F32),
+                *[pltpu.VMEM((2, 2, TILE + 16, TILE), F32)] * 2,
+                *[pltpu.VMEM((2, 2 * TILE, 2 * TILE), BF16)] * 2,
+                *[pltpu.VMEM((2, 2 * TILE, 2 * TILE), F32)] * 2,
+                pltpu.VMEM((2, 2, longest * TILE + 2 * HALO, TILE), F32),
                 pltpu.VMEM((2, sum(count for _, count in runs) * TILE, TILE), F32),
                 pltpu.SemaphoreType.DMA,
             ],

time: 66.8 us -> 62.1 us (0.930)
  Pallas kernels: 31.9 us -> 25.9 us
  starting transfers between devices: 22.4 us -> 25 us
  waiting for transfers between devices: 11.9 us -> 10.5 us
    pallas_call x8 -> x7, Pallas kernels: 31.9 us -> 25.9 us  [call(): return pl.pallas_call(kernel, compiler_params=PARAMS, **settings)(*operands)]
    ppermute x12, starting transfers between devices: 17.1 us -> 19.7 us  [swap(): return lax.ppermute(block, 'aper', [(i, i ^ k) for i in range(apers)])]
    ppermute x12, waiting for transfers between devices: 10.9 us -> 9.55 us  [swap(): return lax.ppermute(block, 'aper', [(i, i ^ k) for i in range(apers)])]
  transfers between devices with their start and end apart: 15 -> 15, of which waited for: 6 -> 5; matrix products, arithmetic and copies ran while one was open for 0% -> 0% of each run, Pallas kernels for 26% -> 24%
where the time goes in v1:
time: 62.1 us; the launch traced here: 61.9 us
  Pallas kernels  25.9 us (42%)
  starting transfers between devices  25 us (40%)
  waiting for transfers between devices  10.5 us (17%)
    pallas_call x7, Pallas kernels, call(): return pl.pallas_call(kernel, compiler_params=PARAMS, **settings)(*operands)  25.9 us
    ppermute x12, starting transfers between devices, swap(): return lax.ppermute(block, 'aper', [(i, i ^ k) for i in range(apers)])  19.7 us
    ppermute x12, waiting for transfers between devices, swap(): return lax.ppermute(block, 'aper', [(i, i ^ k) for i in range(apers)])  9.55 us
    ppermute x1, starting transfers between devices, body(): low = lax.ppermute(to_high, 'rng', [(i, i + 1) for i in range(ranks - 1)])  3.49 us
    ppermute x1, starting transfers between devices, body(): high = lax.ppermute(to_low, 'rng', [(i + 1, i) for i in range(ranks - 1)])  1.29 us
  transfers between devices with their start and end apart: 15, of which 5 were waited for; matrix products, arithmetic and copies ran while one was open for 0% of the time, Pallas kernels for 24%

profile of v1, /device:TPU:0, one launch (start us, length us, event | category | flops | bytes accessed | tf_op | source)
XLA Modules:
  0.0 61.9 jit_solution(6202313921182195105)
XLA Ops:
  0.0 0.1 pad_add_fusion.sc
  0.1 2.5 %shard_map.127 = (f32[2,32,512]{2,1,0:T(8,128)S(1)}, f32[2,32,512]{2,1,0:T(8,128)S(1)}, f32[2,32,512]{2,1,0:T(8,128)S(1)}, f32[2,8,2048]{2,1,0:T(8,128)S(1)}, f32[2,128,2048]{2,1,0:T(8,128)S(1)}) custom-call(s32[4]{0:T(128)S(1)} %pad_add_fusion.sc, f32[1,2,2048,128]{3,2,1,0:T(8,128)} %child.1), custom_call_target="tpu_custom_call" | custom-call | tf_op jit(solution)/shard_map/pallas_call | solution.py:491
  2.5 0.6 collective-permute-start
  3.1 1.0 %collective-permute-done.rim = f32[2,8,2048]{2,1,0:T(8,128)S(1)} collective-permute-done((f32[2,8,2048]{2,1,0:T(8,128)S(1)}, f32[2,8,2048]{2,1,0:T(8,128)S(1)}, u32[]{:S(2)}, u32[]{:S(2)}) %collective-permute-start) | collective-permute-done | bytes 131104 | tf_op jit(solution)/shard_map/ppermute | solution.py:508
  4.1 0.0 copy-start.5
  4.1 0.0 copy-start.6
  4.1 0.0 copy-start.7
  4.1 0.0 copy-start.8
  4.2 0.0 copy-start.10
  4.2 0.0 copy-start.11
  4.2 0.9 %shard_map.128 = (f32[2,64,512]{2,1,0:T(8,128)S(1)}, f32[2,64,512]{2,1,0:T(8,128)S(1)}, f32[2,64,512]{2,1,0:T(8,128)S(1)}, f32[2,48,512]{2,1,0:T(8,128)S(1)}, f3...) custom-call(s32[4]{0:T(128)S(1)} %pad_add_fusion.sc, ...), custom_call_target="tpu_custom_call" | custom-call | tf_op jit(solution)/shard_map/pallas_call | solution.py:491
  5.1 2.9 %collective-permute-start.4 = (f32[2,64,512]{2,1,0:T(8,128)S(1)}, f32[2,64,512]{2,1,0:T(8,128)S(1)}, u32[]{:S(2)}, u32[]{:S(2)}) collective-permute-start(f32[2,64,512]{2,1,0:T(8,128)S(1)} %get-tuple-element.37), channel_id=1, source_target_pairs={{0,8},{8,0},{16,24},{24,16},{1,9},{9,1},{17,25},{25,17},{2,10},{10... | collective-permute-start | bytes 786440 | tf_op jit(solution)/shard_map/ppermute | solution.py:494
  8.0 0.1 collective-permute-start.1
  8.1 2.0 %collective-permute-start.2 = (f32[2,32,512]{2,1,0:T(8,128)S(1)}, f32[2,32,512]{2,1,0:T(8,128)S(1)}, u32[]{:S(2)}, u32[]{:S(2)}) collective-permute-start(f32[2,32,512]{2,1,0:T(8,128)S(1)} %get-tuple-element.35), channel_id=1, source_target_pairs={{0,16},{8,24},{16,0},{24,8},{1,17},{9,25},{17,1},{25,9},{2,18},{10... | collective-permute-start | bytes 393224 | tf_op jit(solution)/shard_map/ppermute | solution.py:494
  10.0 1.4 %collective-permute-start.3 = (f32[2,32,512]{2,1,0:T(8,128)S(1)}, f32[2,32,512]{2,1,0:T(8,128)S(1)}, u32[]{:S(2)}, u32[]{:S(2)}) collective-permute-start(f32[2,32,512]{2,1,0:T(8,128)S(1)} %get-tuple-element.36), channel_id=1, source_target_pairs={{0,24},{8,16},{16,8},{24,0},{1,25},{9,17},{17,9},{25,1},{2,26},{10... | collective-permute-start | bytes 393224 | tf_op jit(solution)/shard_map/ppermute | solution.py:494
  11.5 1.5 %collective-permute-start.5 = (f32[2,64,512]{2,1,0:T(8,128)S(1)}, f32[2,64,512]{2,1,0:T(8,128)S(1)}, u32[]{:S(2)}, u32[]{:S(2)}) collective-permute-start(f32[2,64,512]{2,1,0:T(8,128)S(1)} %get-tuple-element.38), channel_id=1, source_target_pairs={{0,16},{8,24},{16,0},{24,8},{1,17},{9,25},{17,1},{25,9},{2,18},{10... | collective-permute-start | bytes 786440 | tf_op jit(solution)/shard_map/ppermute | solution.py:494
  13.0 5.0 %collective-permute-done.1.refs_0_.refs_1_.refs_3_ = f32[2,32,512]{2,1,0:T(8,128)S(1)} collective-permute-done((f32[2,32,512]{2,1,0:T(8,128)S(1)}, f32[2,32,512]{2,1,0:T(8,128)S(1)}, u32[]{:S(2)}, u32[]{:S(2)}) %collective-permute-start.1) | collective-permute-done | bytes 131104 | tf_op jit(solution)/shard_map/ppermute | solution.py:494
  17.9 3.0 %collective-permute-start.6 = (f32[2,64,512]{2,1,0:T(8,128)S(1)}, f32[2,64,512]{2,1,0:T(8,128)S(1)}, u32[]{:S(2)}, u32[]{:S(2)}) collective-permute-start(f32[2,64,512]{2,1,0:T(8,128)S(1)} %get-tuple-element.39), channel_id=1, source_target_pairs={{0,24},{8,16},{16,8},{24,0},{1,25},{9,17},{17,9},{25,1},{2,26},{10... | collective-permute-start | bytes 786440 | tf_op jit(solution)/shard_map/ppermute | solution.py:494
  20.9 0.5 collective-permute-start.7
  21.5 0.9 %collective-permute-done.3.refs_2_.refs_3_.refs_5_ = f32[2,32,512]{2,1,0:T(8,128)S(1)} collective-permute-done((f32[2,32,512]{2,1,0:T(8,128)S(1)}, f32[2,32,512]{2,1,0:T(8,128)S(1)}, u32[]{:S(2)}, u32[]{:S(2)}) %collective-permute-start.3) | collective-permute-done | bytes 131104 | tf_op jit(solution)/shard_map/ppermute | solution.py:494
  22.3 3.0 %collective-permute-start.9 = (f32[2,48,512]{2,1,0:T(8,128)S(1)}, f32[2,48,512]{2,1,0:T(8,128)S(1)}, u32[]{:S(2)}, u32[]{:S(2)}) collective-permute-start(f32[2,48,512]{2,1,0:T(8,128)S(1)} %get-tuple-element.42), channel_id=1, source_target_pairs={{0,24},{8,16},{16,8},{24,0},{1,25},{9,17},{17,9},{25,1},{2,26},{10... | collective-permute-start | bytes 589832 | tf_op jit(solution)/shard_map/ppermute | solution.py:494
  25.3 3.6 %collective-permute-done.5.refs_4_.refs_5_.refs_7_ = f32[2,64,512]{2,1,0:T(8,128)S(1)} collective-permute-done((f32[2,64,512]{2,1,0:T(8,128)S(1)}, f32[2,64,512]{2,1,0:T(8,128)S(1)}, u32[]{:S(2)}, u32[]{:S(2)}) %collective-permute-start.5) | collective-permute-done | bytes 262176 | tf_op jit(solution)/shard_map/ppermute | solution.py:494
  28.9 1.2 %collective-permute-start.10 = (f32[2,48,512]{2,1,0:T(8,128)S(1)}, f32[2,48,512]{2,1,0:T(8,128)S(1)}, u32[]{:S(2)}, u32[]{:S(2)}) collective-permute-start(f32[2,48,512]{2,1,0:T(8,128)S(1)} %get-tuple-element.43), channel_id=1, source_target_pairs={{0,8},{8,0},{16,24},{24,16},{1,9},{9,1},{17,25},{25,17},{2,10},{10... | collective-permute-start | bytes 589832 | tf_op jit(solution)/shard_map/ppermute | solution.py:494
  30.1 3.5 %collective-permute-start.13 = (f32[4,2,48,128]{3,2,1,0:T(8,128)S(1)}, f32[4,2,48,128]{3,2,1,0:T(8,128)S(1)}, u32[]{:S(2)}, u32[]{:S(2)}) collective-permute-start(f32[4,2,48,128]{3,2,1,0:T(8,128)S(1)} %get-tuple-element.55), channel_id=1, source_target_pairs={{0,2},{2,4},{4,6},{1,3},{3,5},{5,7},{8,10},{10,12},{12,14},{9,11},... | collective-permute-start | bytes 589832 | tf_op jit(solution)/shard_map/ppermute | solution.py:531
  33.6 1.3 %collective-permute-start.14 = (f32[4,2,48,128]{3,2,1,0:T(8,128)S(1)}, f32[4,2,48,128]{3,2,1,0:T(8,128)S(1)}, u32[]{:S(2)}, u32[]{:S(2)}) collective-permute-start(f32[4,2,48,128]{3,2,1,0:T(8,128)S(1)} %get-tuple-element.56), channel_id=1, source_target_pairs={{2,0},{4,2},{6,4},{3,1},{5,3},{7,5},{10,8},{12,10},{14,12},{11,9},... | collective-permute-start | bytes 589832 | tf_op jit(solution)/shard_map/ppermute | solution.py:532
  34.9 0.1 collective-permute-done.8.refs_10_.refs_8_
  35.0 2.9 %collective-permute-start.11 = (f32[2,48,512]{2,1,0:T(8,128)S(1)}, f32[2,48,512]{2,1,0:T(8,128)S(1)}, u32[]{:S(2)}, u32[]{:S(2)}) collective-permute-start(f32[2,48,512]{2,1,0:T(8,128)S(1)} %get-tuple-element.44), channel_id=1, source_target_pairs={{0,16},{8,24},{16,0},{24,8},{1,17},{9,25},{17,1},{25,9},{2,18},{10... | collective-permute-start | bytes 589832 | tf_op jit(solution)/shard_map/ppermute | solution.py:494
  38.0 1.2 %collective-permute-start.12 = (f32[2,48,512]{2,1,0:T(8,128)S(1)}, f32[2,48,512]{2,1,0:T(8,128)S(1)}, u32[]{:S(2)}, u32[]{:S(2)}) collective-permute-start(f32[2,48,512]{2,1,0:T(8,128)S(1)} %get-tuple-element.45), channel_id=1, source_target_pairs={{0,24},{8,16},{16,8},{24,0},{1,25},{9,17},{17,9},{25,1},{2,26},{10... | collective-permute-start | bytes 589832 | tf_op jit(solution)/shard_map/ppermute | solution.py:494
  39.2 1.4 %shard_map.129 = (f32[2,16,128]{2,1,0:T(8,128)S(1)}, bf16[2,256,256]{2,1,0:T(8,128)(2,1)S(1)}, bf16[2,128,256]{2,1,0:T(8,128)(2,1)S(1)}, f32[2,2,24,128]{3,2,1,0...) custom-call(s32[4]{0:T(128)S(1)} %pad_add_fusion.sc, ...), custom_call_target="tpu_custom_call" | custom-call | tf_op jit(solution)/shard_map/pallas_call | solution.py:491
  40.7 5.6 %shard_map.131.refs_21_ = f32[1,2,2048,128]{3,2,1,0:T(8,128)} custom-call(s32[4]{0:T(128)S(1)} %pad_add_fusion.sc, f32[2,48,2048]{2,1,0:T(8,128)S(1)} %get-tuple-element.33.own.refs_0_, f32[2,32,512]{2,1,0:T(8,128)S(1)} %collective-permute-done.1.refs_0_.refs_1_.refs_3_, f32[2,32,512]{2,1,0:T(8,128)S(1)} %collective-permute-done.2.refs_1_.refs_2_.refs_4_, ...), custom_call_target="tpu_custom_call" | custom-call | tf_op jit(solution)/shard_map/pallas_call | solution.py:491
  46.3 7.9 %shard_map.132.refs_22_ = f32[1,2,2048,128]{3,2,1,0:T(8,128)} custom-call(s32[4]{0:T(128)S(1)} %pad_add_fusion.sc, f32[2,48,2048]{2,1,0:T(8,128)S(1)} %get-tuple-element.33.own.refs_0_, f32[4,2,48,128]{3,2,1,0:T(8,128)S(1)} %collective-permute-done.13.refs_1_, ...), custom_call_target="tpu_custom_call", output_to_operand_aliasing={{}: (22, {})} | custom-call | tf_op jit(solution)/shard_map/pallas_call | solution.py:491
  54.2 7.7 %shard_map.133 = f32[1,2,2048,128]{3,2,1,0:T(8,128)} custom-call(s32[4]{0:T(128)S(1)} %pad_add_fusion.sc, f32[2,48,2048]{2,1,0:T(8,128)S(1)} %get-tuple-element.33.own.refs_0_, f32[2,32,512]{2,1,0:T(8,128)S(1)} %collective-permute-done.1.refs_0_.refs_1_.refs_3_, ...), custom_call_target="tpu_custom_call", output_to_operand_aliasing={{}: (23, {})} | custom-call | tf_op jit(solution)/shard_map/pallas_call | solution.py:491
  (30 shorter events, 0.1 us)
Async XLA Ops:
  2.5 1.5 %collective-permute-start = (f32[2,8,2048]{2,1,0:T(8,128)S(1)}, f32[2,8,2048]{2,1,0:T(8,128)S(1)}, u32[]{:S(2)}, u32[]{:S(2)}) collective-permute-start(f32[2,8,2048]{2,1,0:T(8,128)S(1)} %get-tuple-element.32), channel_id=1, source_target_pairs={{0,1},{1,0},{2,3},{3,2},{4,5},{5,4},{6,7},{7,6},{8,9},{9,8},{10,11... | collective-permute-start | bytes 393224 | tf_op jit(solution)/shard_map/ppermute | solution.py:508
  4.1 35.1 %copy-start = (f32[2,8,1024]{2,1,0:T(8,128)S(1)}, f32[2,8,1024]{2,1,0:T(8,128)}, u32[]{:S(2)}) copy-start(f32[2,8,1024]{2,1,0:T(8,128)} %btaps_two.1) | copy-start | bytes 196612
  4.1 35.1 %copy-start.1 = (f32[2,8,512]{2,1,0:T(8,128)S(1)}, f32[2,8,512]{2,1,0:T(8,128)}, u32[]{:S(2)}) copy-start(f32[2,8,512]{2,1,0:T(8,128)} %btaps_one.1) | copy-start | bytes 98308
  4.1 35.1 %copy-start.2 = (f32[2,8,512]{2,1,0:T(8,128)S(1)}, f32[2,8,512]{2,1,0:T(8,128)}, u32[]{:S(2)}) copy-start(f32[2,8,512]{2,1,0:T(8,128)} %rtaps_two.1) | copy-start | bytes 98308
  4.1 35.1 %copy-start.3 = (f32[2,8,256]{2,1,0:T(8,128)S(1)}, f32[2,8,256]{2,1,0:T(8,128)}, u32[]{:S(2)}) copy-start(f32[2,8,256]{2,1,0:T(8,128)} %rtaps_one.1) | copy-start | bytes 49156
  4.1 35.1 %copy-start.4 = (s32[2,1024]{1,0:T(2,128)S(1)}, s32[2,1024]{1,0:T(2,128)}, u32[]{:S(2)}) copy-start(s32[2,1024]{1,0:T(2,128)} %bstart_two.1) | copy-start | bytes 24580
  4.1 35.1 %copy-start.5 = (f32[2,1024]{1,0:T(2,128)S(1)}, f32[2,1024]{1,0:T(2,128)}, u32[]{:S(2)}) copy-start(f32[2,1024]{1,0:T(2,128)} %prate_two.1) | copy-start | bytes 24580
  4.1 35.1 %copy-start.6 = (f32[2,1024]{1,0:T(2,128)S(1)}, f32[2,1024]{1,0:T(2,128)}, u32[]{:S(2)}) copy-start(f32[2,1024]{1,0:T(2,128)} %poff_two.1) | copy-start | bytes 24580
  4.1 35.1 %copy-start.7 = (s32[2,512]{1,0:T(2,128)S(1)}, s32[2,512]{1,0:T(2,128)}, u32[]{:S(2)}) copy-start(s32[2,512]{1,0:T(2,128)} %bstart_one.1) | copy-start | bytes 12292
  4.1 35.1 %copy-start.8 = (f32[2,512]{1,0:T(2,128)S(1)}, f32[2,512]{1,0:T(2,128)}, u32[]{:S(2)}) copy-start(f32[2,512]{1,0:T(2,128)} %prate_one.1) | copy-start | bytes 12292
  4.1 35.1 %copy-start.9 = (f32[2,512]{1,0:T(2,128)S(1)}, f32[2,512]{1,0:T(2,128)}, u32[]{:S(2)}) copy-start(f32[2,512]{1,0:T(2,128)} %poff_one.1) | copy-start | bytes 12292
  4.2 35.1 %copy-start.10 = (s32[2,512]{1,0:T(2,128)S(1)}, s32[2,512]{1,0:T(2,128)}, u32[]{:S(2)}) copy-start(s32[2,512]{1,0:T(2,128)} %shift_two.1) | copy-start | bytes 12292
  4.2 35.1 %copy-start.11 = (s32[2,256]{1,0:T(2,128)S(1)}, s32[2,256]{1,0:T(2,128)}, u32[]{:S(2)}) copy-start(s32[2,256]{1,0:T(2,128)} %shift_one.1) | copy-start | bytes 6148
  5.1 17.3 %collective-permute-start.4 = (f32[2,64,512]{2,1,0:T(8,128)S(1)}, f32[2,64,512]{2,1,0:T(8,128)S(1)}, u32[]{:S(2)}, u32[]{:S(2)}) collective-permute-start(f32[2,64,512]{2,1,0:T(8,128)S(1)} %get-tuple-element.37), channel_id=1, source_target_pairs={{0,8},{8,0},{16,24},{24,16},{1,9},{9,1},{17,25},{25,17},{2,10},{10... | collective-permute-start | bytes 786440 | tf_op jit(solution)/shard_map/ppermute | solution.py:494
  8.0 10.0 %collective-permute-start.1 = (f32[2,32,512]{2,1,0:T(8,128)S(1)}, f32[2,32,512]{2,1,0:T(8,128)S(1)}, u32[]{:S(2)}, u32[]{:S(2)}) collective-permute-start(f32[2,32,512]{2,1,0:T(8,128)S(1)} %get-tuple-element.34), channel_id=1, source_target_pairs={{0,8},{8,0},{16,24},{24,16},{1,9},{9,1},{17,25},{25,17},{2,10},{10... | collective-permute-start | bytes 393224 | tf_op jit(solution)/shard_map/ppermute | solution.py:494
  8.1 12.9 %collective-permute-start.2 = (f32[2,32,512]{2,1,0:T(8,128)S(1)}, f32[2,32,512]{2,1,0:T(8,128)S(1)}, u32[]{:S(2)}, u32[]{:S(2)}) collective-permute-start(f32[2,32,512]{2,1,0:T(8,128)S(1)} %get-tuple-element.35), channel_id=1, source_target_pairs={{0,16},{8,24},{16,0},{24,8},{1,17},{9,25},{17,1},{25,9},{2,18},{10... | collective-permute-start | bytes 393224 | tf_op jit(solution)/shard_map/ppermute | solution.py:494
  10.0 12.3 %collective-permute-start.3 = (f32[2,32,512]{2,1,0:T(8,128)S(1)}, f32[2,32,512]{2,1,0:T(8,128)S(1)}, u32[]{:S(2)}, u32[]{:S(2)}) collective-permute-start(f32[2,32,512]{2,1,0:T(8,128)S(1)} %get-tuple-element.36), channel_id=1, source_target_pairs={{0,24},{8,16},{16,8},{24,0},{1,25},{9,17},{17,9},{25,1},{2,26},{10... | collective-permute-start | bytes 393224 | tf_op jit(solution)/shard_map/ppermute | solution.py:494
  11.5 17.4 %collective-permute-start.5 = (f32[2,64,512]{2,1,0:T(8,128)S(1)}, f32[2,64,512]{2,1,0:T(8,128)S(1)}, u32[]{:S(2)}, u32[]{:S(2)}) collective-permute-start(f32[2,64,512]{2,1,0:T(8,128)S(1)} %get-tuple-element.38), channel_id=1, source_target_pairs={{0,16},{8,24},{16,0},{24,8},{1,17},{9,25},{17,1},{25,9},{2,18},{10... | collective-permute-start | bytes 786440 | tf_op jit(solution)/shard_map/ppermute | solution.py:494
  17.9 12.1 %collective-permute-start.6 = (f32[2,64,512]{2,1,0:T(8,128)S(1)}, f32[2,64,512]{2,1,0:T(8,128)S(1)}, u32[]{:S(2)}, u32[]{:S(2)}) collective-permute-start(f32[2,64,512]{2,1,0:T(8,128)S(1)} %get-tuple-element.39), channel_id=1, source_target_pairs={{0,24},{8,16},{16,8},{24,0},{1,25},{9,17},{17,9},{25,1},{2,26},{10... | collective-permute-start | bytes 786440 | tf_op jit(solution)/shard_map/ppermute | solution.py:494
  20.9 12.7 %collective-permute-start.7 = (f32[2,48,512]{2,1,0:T(8,128)S(1)}, f32[2,48,512]{2,1,0:T(8,128)S(1)}, u32[]{:S(2)}, u32[]{:S(2)}) collective-permute-start(f32[2,48,512]{2,1,0:T(8,128)S(1)} %get-tuple-element.40), channel_id=1, source_target_pairs={{0,8},{8,0},{16,24},{24,16},{1,9},{9,1},{17,25},{25,17},{2,10},{10... | collective-permute-start | bytes 589832 | tf_op jit(solution)/shard_map/ppermute | solution.py:494
  22.3 12.7 %collective-permute-start.8 = (f32[2,48,512]{2,1,0:T(8,128)S(1)}, f32[2,48,512]{2,1,0:T(8,128)S(1)}, u32[]{:S(2)}, u32[]{:S(2)}) collective-permute-start(f32[2,48,512]{2,1,0:T(8,128)S(1)} %get-tuple-element.41), channel_id=1, source_target_pairs={{0,16},{8,24},{16,0},{24,8},{1,17},{9,25},{17,1},{25,9},{2,18},{10... | collective-permute-start | bytes 589832 | tf_op jit(solution)/shard_map/ppermute | solution.py:494
  22.3 15.6 %collective-permute-start.9 = (f32[2,48,512]{2,1,0:T(8,128)S(1)}, f32[2,48,512]{2,1,0:T(8,128)S(1)}, u32[]{:S(2)}, u32[]{:S(2)}) collective-permute-start(f32[2,48,512]{2,1,0:T(8,128)S(1)} %get-tuple-element.42), channel_id=1, source_target_pairs={{0,24},{8,16},{16,8},{24,0},{1,25},{9,17},{17,9},{25,1},{2,26},{10... | collective-permute-start | bytes 589832 | tf_op jit(solution)/shard_map/ppermute | solution.py:494
  28.9 25.3 %collective-permute-start.10 = (f32[2,48,512]{2,1,0:T(8,128)S(1)}, f32[2,48,512]{2,1,0:T(8,128)S(1)}, u32[]{:S(2)}, u32[]{:S(2)}) collective-permute-start(f32[2,48,512]{2,1,0:T(8,128)S(1)} %get-tuple-element.43), channel_id=1, source_target_pairs={{0,8},{8,0},{16,24},{24,16},{1,9},{9,1},{17,25},{25,17},{2,10},{10... | collective-permute-start | bytes 589832 | tf_op jit(solution)/shard_map/ppermute | solution.py:494
  30.1 16.1 %collective-permute-start.13 = (f32[4,2,48,128]{3,2,1,0:T(8,128)S(1)}, f32[4,2,48,128]{3,2,1,0:T(8,128)S(1)}, u32[]{:S(2)}, u32[]{:S(2)}) collective-permute-start(f32[4,2,48,128]{3,2,1,0:T(8,128)S(1)} %get-tuple-element.55), channel_id=1, source_target_pairs={{0,2},{2,4},{4,6},{1,3},{3,5},{5,7},{8,10},{10,12},{12,14},{9,11},... | collective-permute-start | bytes 589832 | tf_op jit(solution)/shard_map/ppermute | solution.py:531
  33.6 12.6 %collective-permute-start.14 = (f32[4,2,48,128]{3,2,1,0:T(8,128)S(1)}, f32[4,2,48,128]{3,2,1,0:T(8,128)S(1)}, u32[]{:S(2)}, u32[]{:S(2)}) collective-permute-start(f32[4,2,48,128]{3,2,1,0:T(8,128)S(1)} %get-tuple-element.56), channel_id=1, source_target_pairs={{2,0},{4,2},{6,4},{3,1},{5,3},{7,5},{10,8},{12,10},{14,12},{11,9},... | collective-permute-start | bytes 589832 | tf_op jit(solution)/shard_map/ppermute | solution.py:532
  35.0 19.1 %collective-permute-start.11 = (f32[2,48,512]{2,1,0:T(8,128)S(1)}, f32[2,48,512]{2,1,0:T(8,128)S(1)}, u32[]{:S(2)}, u32[]{:S(2)}) collective-permute-start(f32[2,48,512]{2,1,0:T(8,128)S(1)} %get-tuple-element.44), channel_id=1, source_target_pairs={{0,16},{8,24},{16,0},{24,8},{1,17},{9,25},{17,1},{25,9},{2,18},{10... | collective-permute-start | bytes 589832 | tf_op jit(solution)/shard_map/ppermute | solution.py:494
  38.0 16.2 %collective-permute-start.12 = (f32[2,48,512]{2,1,0:T(8,128)S(1)}, f32[2,48,512]{2,1,0:T(8,128)S(1)}, u32[]{:S(2)}, u32[]{:S(2)}) collective-permute-start(f32[2,48,512]{2,1,0:T(8,128)S(1)} %get-tuple-element.45), channel_id=1, source_target_pairs={{0,24},{8,16},{16,8},{24,0},{1,25},{9,17},{17,9},{25,1},{2,26},{10... | collective-permute-start | bytes 589832 | tf_op jit(solution)/shard_map/ppermute | solution.py:494
